TPU v7x, 32 devices: a whole 2x2x4 slice. The times are simulated.
32 devices in a mesh: groups: 2 (over y), ctx: 4 (over z), head: 2 (over x), rep: 2 (over core).
Axes of the slice: x: 2, y: 2, z: 4, core: 2. Of those that a mesh axis runs over, the one named last changes fastest.
Arguments:
- queries: bfloat16 [2048, 4096], P(('groups', 'ctx'), ('head', 'rep')), parts along dimension 0, may hold values from -24 to 24
- keys: bfloat16 [2048, 1024], P(('groups', 'ctx'), ('head', 'rep')), parts along dimension 0, may hold values from -6 to 6
- values: bfloat16 [2048, 1024], P(('groups', 'ctx'), ('head', 'rep')), parts along dimension 0, may hold values from -6 to 6
- span_order: int32 [8], replicated, may hold values from 0 to 7, as said below
Outputs:
- attended: bfloat16 [2048, 4096], P(('groups', 'ctx'), ('head', 'rep')), parts along dimension 0
There are 2 independent parts, one for each index of `groups`. A program takes and returns all parts, laid end to end along the dimension named above; an argument that names none is the same for every part. Nothing has to cross between parts.
Inputs may be any that keep to these rules, and one draw needn't show every extreme that they name: `span_order`: A permutation of the spans in which entries 2 d and 2 d + 1 are c and 7 - c for some c.
All inputs are finite; a program needn't handle non-finite values.
Results may differ from a plain program's by a relative error of at most 0.0047.
Values may be sent and summed in bfloat16 or wider, within the bound.
A program may use at most 64 MiB of HBM per device.

v0:
```python
import math

import jax
import jax.numpy as jnp
from jax import lax
from jax.sharding import PartitionSpec as P

HEAD_SIZE = 128


masked_score = -1e30


def lookup_positions(span_order, first_row, row_count, span_rows):
    row_ids = first_row + jnp.arange(row_count, dtype=jnp.int32)
    span_ids = row_ids // span_rows
    span_table = jnp.arange(span_order.shape[0], dtype=jnp.int32)
    span_starts = jnp.sum(
        jnp.where(span_ids[:, None] == span_table[None, :], span_order[None, :], 0), axis=1
    )
    return span_starts * span_rows + row_ids % span_rows


def source_partials(query_block, query_pos, key_group, value_group, key_pos, head_dim):
    score_scale = 1.0 / math.sqrt(head_dim)
    scores = (
        jnp.einsum("rhgd,cshd->crhgs", query_block, key_group, preferred_element_type=jnp.float32)
        * score_scale
    )
    allowed = (key_pos[:, None, :] <= query_pos[None, :, None])[:, :, None, None, :]
    masked = jnp.where(allowed, scores, masked_score)
    row_top = jnp.max(masked, axis=-1)
    weights = jnp.where(allowed, jnp.exp(masked - row_top[..., None]), 0.0)
    row_total = jnp.sum(weights, axis=-1)
    numerator = jnp.einsum(
        "crhgs,cshd->crhgd",
        weights.astype(jnp.bfloat16),
        value_group,
        preferred_element_type=jnp.float32,
    )
    partial_value = (numerator / jnp.maximum(row_total, 1.0)[..., None]).astype(jnp.bfloat16)
    return (partial_value, row_top, row_total)


def absorb(running, partial_value, row_top, row_total):
    run_top, run_total, run_sum = running
    new_top = jnp.maximum(run_top, row_top)
    rescale = jnp.exp(run_top - new_top)
    source_weight = row_total * jnp.exp(row_top - new_top)
    return (
        new_top,
        run_total * rescale + source_weight,
        run_sum * rescale[..., None] + source_weight[..., None] * partial_value.astype(jnp.float32),
    )


def shards(queries, keys, values, span_order):
    rows_here = queries.shape[0]
    span_rows = rows_here // 2
    head_dim = HEAD_SIZE
    kv_heads = keys.shape[1] // head_dim
    common_values = queries.shape[1] // keys.shape[1]
    my_index = lax.axis_index("ctx")
    own_pos = lookup_positions(span_order, my_index * rows_here, rows_here, span_rows)
    q_local = queries.reshape(rows_here, kv_heads, common_values, head_dim)
    initial = (
        jnp.full((rows_here, kv_heads, common_values), masked_score, jnp.float32),
        jnp.zeros((rows_here, kv_heads, common_values), jnp.float32),
        jnp.zeros((rows_here, kv_heads, common_values, head_dim), jnp.float32),
    )
    running = initial
    k_piece = lax.all_gather(keys, "ctx", axis=0, tiled=True)
    v_piece = lax.all_gather(values, "ctx", axis=0, tiled=True)
    shard_count = k_piece.shape[0] // rows_here
    per_turn = 2
    turn_count = shard_count // per_turn
    k_pos = lookup_positions(span_order, jnp.int32(0), k_piece.shape[0], span_rows)
    k_steps = k_piece.reshape(turn_count, per_turn, rows_here, kv_heads, head_dim)
    v_steps = v_piece.reshape(turn_count, per_turn, rows_here, kv_heads, head_dim)
    p_steps = k_pos.reshape(turn_count, per_turn, rows_here)

    def one_turn(carried, inputs_now):
        partial_value, row_top, row_total = source_partials(
            q_local, own_pos, inputs_now[0], inputs_now[1], inputs_now[2], head_dim
        )
        for member in range(per_turn):
            carried = absorb(carried, partial_value[member], row_top[member], row_total[member])
        return (carried, None)

    running, unused = lax.scan(one_turn, running, (k_steps, v_steps, p_steps))
    merged = running[2] / running[1][..., None]
    return merged.reshape(rows_here, kv_heads * common_values * head_dim).astype(jnp.bfloat16)


def solution(mesh):
    return jax.shard_map(
        shards,
        mesh=mesh,
        in_specs=(
            P(("groups", "ctx"), ("head", "rep")),
            P(("groups", "ctx"), ("head", "rep")),
            P(("groups", "ctx"), ("head", "rep")),
            P(),
        ),
        out_specs=P(("groups", "ctx"), ("head", "rep")),
        check_vma=False,
    )
```

profile of v0, /device:TPU:0, one launch (start us, length us, event | category | flops | bytes accessed | tf_op | source)
XLA Modules:
  0.0 60.6 jit_solution(10825627206917604020)
XLA Ops:
  0.0 0.0 copy-start
  0.0 0.8 %select_reduce_fusion.1 = s32[256]{0:T(256)S(1)} fusion(s32[8]{0:T(128)} %param.9, s32[256]{0:T(256)S(1)} %and_select_fusion.2), kind=kLoop, calls=%fused_computation.45 | loop fusion | flops 5888 | bytes 2080 | tf_op jit(solution)/shard_map/reduce_sum | solution.py:18
  0.8 1.2 %copy.30 = bf16[256,1024]{0,1:T(8,128)(2,1)S(1)} copy(bf16[256,1024]{1,0:T(8,128)(2,1)} %param.6) | data formatting | bytes 1048576 | tf_op args[0]
  2.1 1.0 %copy.32 = bf16[256,2,4,128]{3,0,2,1:T(8,128)(2,1)} copy(bf16[256,2,4,128]{0,3,2,1:T(8,128)(2,1)S(1)} %bitcast.99) | data formatting | bytes 1048576
  3.1 17.6 %all_gather.6 = bf16[1024,256]{1,0:T(8,128)(2,1)S(1)} all-gather(bf16[256,256]{1,0:T(8,128)(2,1)} %param.7), channel_id=1, replica_groups=mesh['groups'=2,'ctx'=4,'head'=2,'rep'=2] {'ctx'}, dimensions={0}, use_global_device_ids=true | all-gather | bytes 655360 | tf_op jit(solution)/shard_map/all_gather | solution.py:72
  20.7 0.9 %reshape.66 = bf16[2,2,256,2,128]{4,3,2,1,0:T(2,128)(2,1)} reshape(bf16[1024,256]{1,0:T(8,128)(2,1)S(1)} %all_gather.6) | data formatting | bytes 1048576 | tf_op jit(solution)/shard_map/reshape | solution.py:78
  21.6 16.6 %all_gather.7 = bf16[1024,256]{1,0:T(8,128)(2,1)S(1)} all-gather(bf16[256,256]{1,0:T(8,128)(2,1)} %param.8), channel_id=1, replica_groups=mesh['groups'=2,'ctx'=4,'head'=2,'rep'=2] {'ctx'}, dimensions={0}, use_global_device_ids=true | all-gather | bytes 655360 | tf_op jit(solution)/shard_map/all_gather | solution.py:73
  38.2 0.9 %reshape.68 = bf16[2,2,256,2,128]{4,3,2,1,0:T(2,128)(2,1)} reshape(bf16[1024,256]{1,0:T(8,128)(2,1)S(1)} %all_gather.7) | data formatting | bytes 1048576 | tf_op jit(solution)/shard_map/reshape | solution.py:79
  39.1 0.0 copy-done
  39.1 0.1 select_reduce_fusion
  39.3 20.2 %while.15 = (s32[]{:T(128)}, f32[256,2,4]{0,2,1:T(4,128)S(1)}, f32[256,2,4]{0,2,1:T(4,128)S(1)}, f32[256,2,4,128]{0,3,2,1:T(8,128)S(1)}, s32[2,2,256]{2,1,0:T(2,...) while((s32[]{:T(128)}, f32[256,2,4]{0,2,1:T(4,128)S(1)}, ...), condition=%wide.region_5.6_spmd.clone, body=%wide.region_2.5_spmd.clone.sunk | while | flops 549871616 | bytes 19995776 | solution.py:90
  39.3 1.4 %constant_dynamic-slice_fusion.3 = (bf16[1,2,256,2,128]{4,3,2,1,0:T(2,128)(2,1)S(1)}, bf16[1,2,256,2,128]{4,3,2,1,0:T(2,128)(2,1)S(1)}) fusion(bf16[2,2,256,2,128]{4,3,2,1,0:T(2,128)(2,1)} %get-tuple-element.251, s32[]{:T(128)} %get-tuple-element.232, bf16[2,2,256,2,128]{4,3,2,1,0:T(2,128)(2,1)} %get-tuple-element.249), kind=kLoop, calls=%fused_computation.38.clone.1 | loop fusion | bytes 1048580 | tf_op jit(solution)/shard_map/while/body/jit(dynamic_index_in_dim)/dynamic_slice | solution.py:90
  40.7 0.1 broadcast_compare_fusion.3
  40.8 1.9 %fusion.43 = (f32[2,256,2,4]{1,3,0,2:T(4,128)S(1)}, f32[2,2,256,256,4]{3,2,4,1,0:T(8,128)S(1)}) fusion(pred[2,256,256]{1,2,0:T(8,128)(4,1)S(1)} %broadcast_compare_fusion.3, bf16[256,2,4,128]{3,0,2,1:T(8,128)(2,1)} %get-tuple-element.250, bf16[1,2,256,2,128]{4,3,2,1,0:T(2,128)(2,1)S(1)} %get-tuple-element.209), kind=kOutput, calls=%fused_computation.2.clone.1 | convolution fusion | flops 271577088 | bytes 5128192 | tf_op jit(solution)/shard_map/while/body/eval_jaxpr/rhgd,cshd->crhgs/dot_general | solution.py:27
  42.7 1.2 %fusion.44 = (bf16[2,256,2,4,256]{1,4,3,0,2:T(8,128)(2,1)S(1)}, f32[2,256,2,4]{1,3,0,2:T(4,128)S(1)}) fusion(f32[2,2,256,256,4]{3,2,4,1,0:T(8,128)S(1)} %get-tuple-element.211, f32[2,256,2,4]{1,3,0,2:T(4,128)S(1)} %get-tuple-element.210, pred[2,256,256]{1,2,0:T(8,128)(4,1)S(1)} %broadcast_compare_fusion.3), kind=kLoop, calls=%fused_computation.3.clone.1 | loop fusion | flops 6287360 | bytes 6455296 | tf_op jit(solution)/shard_map/while/body/eval_jaxpr/convert_element_type | solution.py:37
  43.9 0.9 %copy.63 = bf16[1,2,256,2,128]{2,4,3,1,0:T(8,128)(2,1)} copy(bf16[1,2,256,2,128]{4,3,2,1,0:T(2,128)(2,1)S(1)} %get-tuple-element.216) | data formatting | bytes 524288 | tf_op jit(solution)/shard_map/while/body/jit(dynamic_index_in_dim)/dynamic_slice | solution.py:90
  44.8 2.4 %fusion.46 = bf16[2,256,2,4,128]{1,4,3,2,0:T(8,128)(2,1)} fusion(bf16[2,256,2,4,256]{1,4,3,0,2:T(8,128)(2,1)S(1)} %get-tuple-element.215, bf16[1,2,256,2,128]{2,4,3,1,0:T(8,128)(2,1)} %copy.63, f32[2,256,2,4]{1,3,0,2:T(4,128)S(1)} %get-tuple-element.212), kind=kOutput, calls=%fused_computation.6.clone.1 | convolution fusion | flops 269488128 | bytes 3424256 | tf_op jit(solution)/shard_map/while/body/eval_jaxpr/crhgs,cshd->crhgd/dot_general | solution.py:35
  47.2 2.1 %fusion.47 = f32[256,2,4,128]{0,3,2,1:T(8,128)S(1)} fusion(f32[256,2,4,128]{0,3,2,1:T(8,128)S(1)} %get-tuple-element.235, bf16[2,256,2,4,128]{1,4,3,2,0:T(8,128)(2,1)} %fusion.46, f32[256,2,4]{0,2,1:T(4,128)S(1)} %get-tuple-element.217, f32[256,2,4]{0,2,1:T(4,128)S(1)} %get-tuple-element.218, f32[256,2,4]{0,2,1:T(4,128)S(1)} %get-tuple-element.219, ...), kind=kLoop, calls=%fused_computation.10.clone.1 | loop fusion | flops 2359296 | bytes 3178497 | tf_op jit(solution)/shard_map/while/body/eval_jaxpr/add | solution.py:53
  49.4 1.4 %constant_dynamic-slice_fusion.3 = (bf16[1,2,256,2,128]{4,3,2,1,0:T(2,128)(2,1)S(1)}, bf16[1,2,256,2,128]{4,3,2,1,0:T(2,128)(2,1)S(1)}) fusion(bf16[2,2,256,2,128]{4,3,2,1,0:T(2,128)(2,1)} %get-tuple-element.251, s32[]{:T(128)} %get-tuple-element.232, bf16[2,2,256,2,128]{4,3,2,1,0:T(2,128)(2,1)} %get-tuple-element.249), kind=kLoop, calls=%fused_computation.38.clone.1 | loop fusion | bytes 1048580 | tf_op jit(solution)/shard_map/while/body/jit(dynamic_index_in_dim)/dynamic_slice | solution.py:90
  50.8 0.1 broadcast_compare_fusion.3
  50.9 1.9 %fusion.43 = (f32[2,256,2,4]{1,3,0,2:T(4,128)S(1)}, f32[2,2,256,256,4]{3,2,4,1,0:T(8,128)S(1)}) fusion(pred[2,256,256]{1,2,0:T(8,128)(4,1)S(1)} %broadcast_compare_fusion.3, bf16[256,2,4,128]{3,0,2,1:T(8,128)(2,1)} %get-tuple-element.250, bf16[1,2,256,2,128]{4,3,2,1,0:T(2,128)(2,1)S(1)} %get-tuple-element.209), kind=kOutput, calls=%fused_computation.2.clone.1 | convolution fusion | flops 271577088 | bytes 5128192 | tf_op jit(solution)/shard_map/while/body/eval_jaxpr/rhgd,cshd->crhgs/dot_general | solution.py:27
  52.8 1.2 %fusion.44 = (bf16[2,256,2,4,256]{1,4,3,0,2:T(8,128)(2,1)S(1)}, f32[2,256,2,4]{1,3,0,2:T(4,128)S(1)}) fusion(f32[2,2,256,256,4]{3,2,4,1,0:T(8,128)S(1)} %get-tuple-element.211, f32[2,256,2,4]{1,3,0,2:T(4,128)S(1)} %get-tuple-element.210, pred[2,256,256]{1,2,0:T(8,128)(4,1)S(1)} %broadcast_compare_fusion.3), kind=kLoop, calls=%fused_computation.3.clone.1 | loop fusion | flops 6287360 | bytes 6455296 | tf_op jit(solution)/shard_map/while/body/eval_jaxpr/convert_element_type | solution.py:37
  54.0 0.9 %copy.63 = bf16[1,2,256,2,128]{2,4,3,1,0:T(8,128)(2,1)} copy(bf16[1,2,256,2,128]{4,3,2,1,0:T(2,128)(2,1)S(1)} %get-tuple-element.216) | data formatting | bytes 524288 | tf_op jit(solution)/shard_map/while/body/jit(dynamic_index_in_dim)/dynamic_slice | solution.py:90
  54.9 2.4 %fusion.46 = bf16[2,256,2,4,128]{1,4,3,2,0:T(8,128)(2,1)} fusion(bf16[2,256,2,4,256]{1,4,3,0,2:T(8,128)(2,1)S(1)} %get-tuple-element.215, bf16[1,2,256,2,128]{2,4,3,1,0:T(8,128)(2,1)} %copy.63, f32[2,256,2,4]{1,3,0,2:T(4,128)S(1)} %get-tuple-element.212), kind=kOutput, calls=%fused_computation.6.clone.1 | convolution fusion | flops 269488128 | bytes 3424256 | tf_op jit(solution)/shard_map/while/body/eval_jaxpr/crhgs,cshd->crhgd/dot_general | solution.py:35
  57.3 2.1 %fusion.47 = f32[256,2,4,128]{0,3,2,1:T(8,128)S(1)} fusion(f32[256,2,4,128]{0,3,2,1:T(8,128)S(1)} %get-tuple-element.235, bf16[2,256,2,4,128]{1,4,3,2,0:T(8,128)(2,1)} %fusion.46, f32[256,2,4]{0,2,1:T(4,128)S(1)} %get-tuple-element.217, f32[256,2,4]{0,2,1:T(4,128)S(1)} %get-tuple-element.218, f32[256,2,4]{0,2,1:T(4,128)S(1)} %get-tuple-element.219, ...), kind=kLoop, calls=%fused_computation.10.clone.1 | loop fusion | flops 2359296 | bytes 3178497 | tf_op jit(solution)/shard_map/while/body/eval_jaxpr/add | solution.py:53
  59.5 0.1 divide_convert_fusion
  59.6 1.0 %copy.39 = bf16[256,1024]{1,0:T(8,128)(2,1)} copy(bf16[256,1024]{0,1:T(8,128)(2,1)S(1)} %bitcast.98) | data formatting | bytes 1048576 | tf_op jit(solution)/shard_map/convert_element_type | solution.py:92
  (13 shorter events, 0.1 us)
Async XLA Ops:
  0.0 39.1 %copy-start = (s32[8]{0:T(128)S(1)}, s32[8]{0:T(128)}, u32[]{:S(2)}) copy-start(s32[8]{0:T(128)} %param.9) | copy-start | bytes 100
where the time goes:
time: 61 us; the launch traced here: 60.6 us
  blocking collectives  34.1 us (56%)
  local copies, waits for them, and re-layouts  9.69 us (16%)
  matrix products  8.65 us (14%)
  other arithmetic  7.94 us (13%)
    all_gather x1, blocking collectives, shards(): k_piece = lax.all_gather(keys, 'ctx', axis=0, tiled=True)  17.6 us
    all_gather x1, blocking collectives, shards(): v_piece = lax.all_gather(values, 'ctx', axis=0, tiled=True)  16.6 us
    dot_general x2, matrix products, source_partials(): jnp.einsum('crhgs,cshd->crhgd', weights.astype(jnp.bfloat16), value_group...  4.85 us
    dynamic_slice x4, local copies, waits for them, and re-layouts, shards(): running, unused = lax.scan(one_turn, running, (k_steps, v_steps, p_steps))  4.53 us
    add x2, other arithmetic, absorb(): run_sum * rescale[..., None]  4.23 us
    dot_general x2, matrix products, source_partials(): jnp.einsum('rhgd,cshd->crhgs', query_block, key_group, preferred_element_...  3.8 us
    convert_element_type x2, other arithmetic, source_partials(): weights.astype(jnp.bfloat16)  2.34 us
    unnamed x4, local copies, waits for them, and re-layouts  2.27 us

commit v1 on v0

v1 whole, which is shorter than its diff:
```python
import functools
import math

import jax
import jax.numpy as jnp
from jax import lax
from jax.experimental import pallas as pl
from jax.experimental.pallas import tpu as pltpu
from jax.sharding import PartitionSpec as P

HEAD_SIZE = 128
MASKED = -1e30
MESH = pl.DeviceIdType.MESH
RIGHT, LEFT = 0, 1
KEY, VALUE = 0, 1


def attend(
    n, order_ref, q_hbm, k_hbm, v_hbm, out_ref,
    q_ref, k_ref, v_ref, p_ref, alpha_ref, top_ref, total_ref, acc_ref,
    load_sem, send_sem, recv_sem,
):
    me = lax.axis_index("ctx")
    rows, q_cols = q_ref.shape
    span = rows // 2
    kv_heads = k_ref.shape[2] // HEAD_SIZE
    group = q_cols // HEAD_SIZE // kv_heads
    exponent_scale = math.log2(math.e) / math.sqrt(HEAD_SIZE)
    buffers = (k_ref, v_ref)

    load_k = pltpu.make_async_copy(k_hbm, k_ref.at[me], load_sem.at[0])
    load_v = pltpu.make_async_copy(v_hbm, v_ref.at[me], load_sem.at[1])
    load_q = pltpu.make_async_copy(q_hbm, q_ref, load_sem.at[2])
    load_k.start()
    load_v.start()
    load_q.start()

    has_right, has_left = me < n - 1, me > 0
    barrier = pltpu.get_barrier_semaphore()

    @pl.when(has_right)
    def _():
        pl.semaphore_signal(barrier, inc=1, device_id={"ctx": me + 1}, device_id_type=MESH)

    @pl.when(has_left)
    def _():
        pl.semaphore_signal(barrier, inc=1, device_id={"ctx": me - 1}, device_id_type=MESH)

    pl.semaphore_wait(barrier, jnp.where(has_right, 1, 0) + jnp.where(has_left, 1, 0))

    def hop(way, kind, step, block, target):
        return pltpu.make_async_remote_copy(
            src_ref=buffers[kind].at[block],
            dst_ref=buffers[kind].at[block],
            send_sem=send_sem.at[way, kind, step],
            recv_sem=recv_sem.at[way, kind, step],
            device_id={"ctx": target},
            device_id_type=MESH,
        )

    def pass_right(kind, step):
        return hop(RIGHT, kind, step, me - step, me + 1)

    def pass_left(kind, step):
        return hop(LEFT, kind, step, me + step, me - 1)

    def arrive(kind, step):
        @pl.when(me - step >= 0)
        def _():
            hop(RIGHT, kind, step - 1, me - step, jnp.minimum(me + 1, n - 1)).wait_recv()

            @pl.when(has_right)
            def _():
                pass_right(kind, step).start()

        @pl.when(me + step < n)
        def _():
            hop(LEFT, kind, step - 1, me + step, jnp.maximum(me - 1, 0)).wait_recv()

            @pl.when(has_left)
            def _():
                pass_left(kind, step).start()

    for kind, load in ((KEY, load_k), (VALUE, load_v)):
        load.wait()

        @pl.when(has_right)
        def _():
            pass_right(kind, 0).start()

        @pl.when(has_left)
        def _():
            pass_left(kind, 0).start()

    load_q.wait()

    def positions(block, axis):
        index = lax.broadcasted_iota(jnp.int32, (rows, rows), axis)
        first, second = order_ref[2 * block], order_ref[2 * block + 1]
        return index + jnp.where(index < span, first * span, second * span - span)

    def columns(head):
        return pl.ds(head * HEAD_SIZE, HEAD_SIZE)

    def weigh(block, slot, opening):
        bias = jnp.where(positions(block, 1) <= positions(me, 0), 0.0, MASKED)
        for head in range(kv_heads * group):
            scores = lax.dot_general(
                q_ref[:, columns(head)], k_ref[block, :, columns(head // group)],
                (((1,), (1,)), ((), ())), preferred_element_type=jnp.float32,
            ) + bias
            top = jnp.max(scores, axis=1, keepdims=True)
            if not opening:
                old = top_ref[head][:, :1]
                top = jnp.maximum(old, top)
                alpha = jnp.exp2((old - top) * exponent_scale)
                alpha_ref[slot, head] = jnp.broadcast_to(alpha, (rows, HEAD_SIZE))
            weights = jnp.exp2((scores - top) * exponent_scale)
            total = jnp.sum(weights, axis=1, keepdims=True)
            if not opening:
                total = total_ref[head][:, :1] * alpha + total
            top_ref[head] = jnp.broadcast_to(top, (rows, HEAD_SIZE))
            total_ref[head] = jnp.broadcast_to(total, (rows, HEAD_SIZE))
            p_ref[slot, head] = weights.astype(jnp.bfloat16)

    def gather(block, slot, opening):
        for head in range(kv_heads * group):
            part = jnp.dot(
                p_ref[slot, head], v_ref[block, :, columns(head // group)],
                preferred_element_type=jnp.float32,
            )
            if not opening:
                part = acc_ref[head] * alpha_ref[slot, head] + part
            acc_ref[head] = part

    weigh(me, 0, True)
    gather(me, 0, True)

    def turn(step, carry):
        def each(work):
            @pl.when(me - step >= 0)
            def _():
                work(me - step, 0, False)

            @pl.when(me + step < n)
            def _():
                work(me + step, 1, False)

        arrive(KEY, step)
        each(weigh)
        arrive(VALUE, step)
        each(gather)
        return carry

    lax.fori_loop(1, n, turn, 0)

    for head in range(kv_heads * group):
        out_ref[:, columns(head)] = (acc_ref[head] / total_ref[head]).astype(out_ref.dtype)

    def drain(step, carry):
        for kind in (KEY, VALUE):
            @pl.when((me - step >= 0) & has_right)
            def _():
                pass_right(kind, step).wait_send()

            @pl.when((me + step < n) & has_left)
            def _():
                pass_left(kind, step).wait_send()
        return carry

    lax.fori_loop(0, n - 1, drain, 0)


def shards(n, queries, keys, values, span_order):
    rows, q_cols = queries.shape
    heads = q_cols // HEAD_SIZE
    per_head = (heads, rows, HEAD_SIZE)
    return pl.pallas_call(
        functools.partial(attend, n),
        out_shape=jax.ShapeDtypeStruct((rows, q_cols), jnp.bfloat16),
        in_specs=[pl.BlockSpec(memory_space=pltpu.SMEM)] + [pl.BlockSpec(memory_space=pl.ANY)] * 3,
        out_specs=pl.BlockSpec(memory_space=pltpu.VMEM),
        scratch_shapes=[
            pltpu.VMEM((rows, q_cols), jnp.bfloat16),
            pltpu.VMEM((n,) + keys.shape, jnp.bfloat16),
            pltpu.VMEM((n,) + values.shape, jnp.bfloat16),
            pltpu.VMEM((2, heads, rows, rows), jnp.bfloat16),
            pltpu.VMEM((2,) + per_head, jnp.float32),
            pltpu.VMEM(per_head, jnp.float32),
            pltpu.VMEM(per_head, jnp.float32),
            pltpu.VMEM(per_head, jnp.float32),
            pltpu.SemaphoreType.DMA((3,)),
            pltpu.SemaphoreType.DMA((2, 2, n)),
            pltpu.SemaphoreType.DMA((2, 2, n)),
        ],
        compiler_params=pltpu.CompilerParams(collective_id=0, has_side_effects=True),
    )(span_order, queries, keys, values)


def solution(mesh):
    split = P(("groups", "ctx"), ("head", "rep"))
    return jax.shard_map(
        functools.partial(shards, mesh.shape["ctx"]),
        mesh=mesh,
        in_specs=(split, split, split, P()),
        out_specs=split,
        check_vma=False,
    )
```

time: 61 us -> 27.7 us (0.45)
  blocking collectives: 34.1 us -> 0 us
  Pallas kernels: 0 us -> 25.7 us
  matrix products: 8.65 us -> 0 us
  other arithmetic: 7.94 us -> 0 us
  local copies, waits for them, and re-layouts: 9.69 us -> 1.87 us
    all_gather x2 -> x0, blocking collectives: 34.1 us -> none  [the longest x1 17.6 us: shards(): k_piece = lax.all_gather(keys, 'ctx', axis=0, tiled=True)]
    pallas_call x0 -> x1, Pallas kernels: none -> 25.7 us  [shards(): pl.pallas_call(functools.partial(attend, n), out_shape=jax.ShapeDtypeStru...]
    dot_general x4 -> x0, matrix products: 8.65 us -> none  [the longest x2 4.85 us: source_partials(): jnp.einsum('crhgs,cshd->crhgd', weights.astype(jnp.bfloat16), value_group...]
    dynamic_slice x4 -> x0, local copies, waits for them, and re-layouts: 4.53 us -> none  [shards(): running, unused = lax.scan(one_turn, running, (k_steps, v_steps, p_steps))]
    add x6 -> x0, other arithmetic: 4.32 us -> none  [the longest x2 4.23 us: absorb(): run_sum * rescale[..., None]]
    convert_element_type x3 -> x0, other arithmetic: 2.44 us -> none  [the longest x2 2.34 us: source_partials(): weights.astype(jnp.bfloat16)]
    reshape x2 -> x0, local copies, waits for them, and re-layouts: 1.85 us -> none  [the longest x1 0.94 us: shards(): v_piece.reshape(turn_count, per_turn, rows_here, kv_heads, head_dim)]
    convert_element_type x1 -> x0, local copies, waits for them, and re-layouts: 1 us -> none  [shards(): merged.reshape(rows_here, kv_heads * common_values * head_dim)]
where the time goes in v1:
time: 27.7 us; the launch traced here: 27.6 us
  Pallas kernels  25.7 us (93%)
  local copies, waits for them, and re-layouts  1.87 us (7%)
    pallas_call x1, Pallas kernels, shards(): pl.pallas_call(functools.partial(attend, n), out_shape=jax.ShapeDtypeStru...  25.7 us
    unnamed x1, local copies, waits for them, and re-layouts  1.87 us

profile of v1, /device:TPU:0, one launch (start us, length us, event | category | flops | bytes accessed | tf_op | source)
XLA Modules:
  0.0 27.6 jit_solution(693026314293423508)
XLA Ops:
  0.0 25.7 %shard_map.46 = bf16[256,1024]{1,0:T(8,128)(2,1)} custom-call(s32[8]{0:T(128)} %order_ref.1, bf16[256,1024]{1,0:T(8,128)(2,1)} %q_hbm.1, bf16[256,256]{1,0:T(8,128)(2,1)} %k_hbm.1, bf16[256,256]{1,0:T(8,128)(2,1)} %v_hbm.1), custom_call_target="tpu_custom_call" | custom-call | tf_op jit(solution)/shard_map/pallas_call | solution.py:178
  25.7 1.9 %copy.6 = bf16[256,1024]{1,0:T(8,128)(2,1)} copy(bf16[256,1024]{1,0:T(8,128)(2,1)} %shard_map.46) | data formatting | bytes 1048576

commit v2 on v1

v2 whole, which is shorter than its diff:
```python
import functools
import math

import jax
import jax.numpy as jnp
from jax import lax
from jax.experimental import pallas as pl
from jax.experimental.pallas import tpu as pltpu
from jax.sharding import PartitionSpec as P

HEAD_SIZE = 128
MASKED = -1e30
MESH = pl.DeviceIdType.MESH
KEY, VALUE = 0, 1


def attend(
    n, order_hbm, q_hbm, k_hbm, v_hbm, out_ref,
    order_ref, q_ref, k_ref, v_ref, stack_ref, p_ref, top_ref, acc_ref,
    load_sem, send_sem, recv_sem,
):
    me = lax.axis_index("ctx")
    rows, q_cols = q_ref.shape
    span = rows // 2
    kv_heads = k_ref.shape[2] // HEAD_SIZE
    group = q_cols // HEAD_SIZE // kv_heads
    exponent_scale = math.log2(math.e) / math.sqrt(HEAD_SIZE)
    buffers = (k_ref, v_ref)

    load_k = pltpu.make_async_copy(k_hbm, k_ref.at[me], load_sem.at[0])
    load_v = pltpu.make_async_copy(v_hbm, v_ref.at[me], load_sem.at[1])
    load_order = pltpu.make_async_copy(order_hbm, order_ref, load_sem.at[3])
    load_q = pltpu.make_async_copy(q_hbm, q_ref, load_sem.at[2])
    load_k.start()
    load_v.start()
    load_q.start()
    load_order.start()

    major = jnp.where(me < n // 2, -1, 1)

    def inside(index):
        return (index >= 0) & (index < n)

    barrier = pltpu.get_barrier_semaphore()
    for way in (-1, 1):
        @pl.when(inside(me + way))
        def _():
            pl.semaphore_signal(barrier, inc=1, device_id={"ctx": me + way}, device_id_type=MESH)

    pl.semaphore_wait(barrier, jnp.where(me > 0, 1, 0) + jnp.where(me < n - 1, 1, 0))

    def hop(way, kind, step, block):
        lane = (way + 1) // 2
        return pltpu.make_async_remote_copy(
            src_ref=buffers[kind].at[block],
            dst_ref=buffers[kind].at[block],
            send_sem=send_sem.at[lane, kind, step],
            recv_sem=recv_sem.at[lane, kind, step],
            device_id={"ctx": jnp.clip(me + way, 0, n - 1)},
            device_id_type=MESH,
        )

    def arrive(kind, step):
        for way in (major, -major):
            @pl.when(inside(me - way * step))
            def _():
                hop(way, kind, step - 1, me - way * step).wait_recv()

                @pl.when(inside(me + way))
                def _():
                    hop(way, kind, step, me - way * step).start()

    for kind, load in ((KEY, load_k), (VALUE, load_v)):
        load.wait()
        for way in (major, -major):
            @pl.when(inside(me + way))
            def _():
                hop(way, kind, 0, me).start()

    load_q.wait()
    load_order.wait()

    def columns(head):
        return pl.ds(head * HEAD_SIZE, HEAD_SIZE)

    def low_first(block):
        return order_ref[2 * block] < order_ref[2 * block + 1]

    def low_span(block):
        return jnp.minimum(order_ref[2 * block], order_ref[2 * block + 1])

    def low_high(ref, block, head):
        first, second = ref[block, :span, columns(head)], ref[block, span:, columns(head)]
        swap = low_first(block)
        return jnp.where(swap, first, second), jnp.where(swap, second, first)

    def score(head, part, keys):
        queries = stack_ref[head, part] if isinstance(part, int) else part
        return lax.dot_general(
            queries, keys, (((1,), (1,)), ((), ())), preferred_element_type=jnp.float32
        )

    def peak(scores):
        return jnp.max(scores, axis=1, keepdims=True)

    def weights_of(scores, top):
        return jnp.exp2((scores - top) * exponent_scale).astype(jnp.bfloat16)

    def keep(ref, value):
        ref[...] = jnp.broadcast_to(value, (group * span, HEAD_SIZE))

    def with_ones(values):
        return jnp.concatenate([values, jnp.ones_like(values)], axis=1)

    def product(weights, values):
        return jnp.dot(weights, with_ones(values), preferred_element_type=jnp.float32)

    mine_first = low_first(me)
    for head in range(kv_heads):
        for member in range(group):
            column = columns(head * group + member)
            first, second = q_ref[:span, column], q_ref[span:, column]
            stack_ref[head, 0, member * span : (member + 1) * span] = jnp.where(mine_first, first, second)
            stack_ref[head, 1, member * span : (member + 1) * span] = jnp.where(mine_first, second, first)

    tall = (group * span, span)
    row = lax.rem(lax.broadcasted_iota(jnp.int32, tall, 0), span)
    bias = jnp.where(lax.broadcasted_iota(jnp.int32, tall, 1) <= row, 0.0, MASKED)
    for head in range(kv_heads):
        key_low, key_high = low_high(k_ref, me, head)
        value_low, value_high = low_high(v_ref, me, head)
        low = score(head, 0, key_low) + bias
        low_top = peak(low)
        keep(top_ref.at[head, 0], low_top)
        acc_ref[head, 0] = product(weights_of(low, low_top), value_low)
        cross = score(head, 1, key_low)
        high = score(head, 1, key_high) + bias
        high_top = jnp.maximum(peak(cross), peak(high))
        keep(top_ref.at[head, 1], high_top)
        acc_ref[head, 1] = product(weights_of(cross, high_top), value_low) + product(
            weights_of(high, high_top), value_high
        )

    def weigh(block):
        earlier = low_span(block) < low_span(me)
        for head in range(kv_heads):
            key_low, key_high = low_high(k_ref, block, head)
            cross = score(head, 1, key_low)
            other = score(
                head,
                jnp.where(earlier, stack_ref[head, 0], stack_ref[head, 1]),
                jnp.where(earlier, key_low, key_high),
            )
            other_top = peak(other)
            old_low, old_high = top_ref[head, 0][:, :1], top_ref[head, 1][:, :1]
            low_top = jnp.maximum(old_low, jnp.where(earlier, other_top, MASKED))
            high_top = jnp.maximum(
                jnp.maximum(old_high, peak(cross)), jnp.where(earlier, MASKED, other_top)
            )
            keep(top_ref.at[head, 0], low_top)
            keep(top_ref.at[head, 1], high_top)
            acc_ref[head, 0] *= jnp.exp2((old_low - low_top) * exponent_scale)
            acc_ref[head, 1] *= jnp.exp2((old_high - high_top) * exponent_scale)
            p_ref[head, 0] = weights_of(cross, high_top)
            p_ref[head, 1] = weights_of(other, jnp.where(earlier, low_top, high_top))

    def gather(block):
        earlier = low_span(block) < low_span(me)
        for head in range(kv_heads):
            value_low, value_high = low_high(v_ref, block, head)
            cross = product(p_ref[head, 0], value_low)
            other = product(p_ref[head, 1], jnp.where(earlier, value_low, value_high))
            acc_ref[head, 0] += jnp.where(earlier, other, 0.0)
            acc_ref[head, 1] += cross + jnp.where(earlier, 0.0, other)

    def turn(step, carry):
        arrive(KEY, step)

        @pl.when(inside(me - major * step))
        def _():
            weigh(me - major * step)

        arrive(VALUE, step)

        @pl.when(inside(me - major * step))
        def _():
            gather(me - major * step)

        @pl.when(inside(me + major * step))
        def _():
            weigh(me + major * step)
            gather(me + major * step)

        return carry

    lax.fori_loop(1, n, turn, 0)

    for head in range(kv_heads):
        for member in range(group):
            column = columns(head * group + member)
            part = pl.ds(member * span, span)
            low = acc_ref[head, 0, part, :HEAD_SIZE] / acc_ref[head, 0, part, HEAD_SIZE:]
            high = acc_ref[head, 1, part, :HEAD_SIZE] / acc_ref[head, 1, part, HEAD_SIZE:]
            out_ref[:span, column] = jnp.where(mine_first, low, high).astype(out_ref.dtype)
            out_ref[span:, column] = jnp.where(mine_first, high, low).astype(out_ref.dtype)

    def drain(step, carry):
        for kind in (KEY, VALUE):
            for way in (major, -major):
                @pl.when(inside(me - way * step) & inside(me + way))
                def _():
                    hop(way, kind, step, me - way * step).wait_send()
        return carry

    lax.fori_loop(0, n - 1, drain, 0)


def shards(n, queries, keys, values, span_order):
    rows, q_cols = queries.shape
    span = rows // 2
    kv_heads = keys.shape[1] // HEAD_SIZE
    tall = q_cols // HEAD_SIZE // kv_heads * span
    inputs = [pltpu.with_memory_space_constraint(x, pltpu.HBM) for x in (span_order, queries, keys, values)]
    return pl.pallas_call(
        functools.partial(attend, n),
        out_shape=jax.ShapeDtypeStruct((rows, q_cols), jnp.bfloat16),
        in_specs=[pl.BlockSpec(memory_space=pltpu.HBM)] * 4,
        out_specs=pl.BlockSpec(memory_space=pltpu.VMEM),
        scratch_shapes=[
            pltpu.SMEM(span_order.shape, jnp.int32),
            pltpu.VMEM((rows, q_cols), jnp.bfloat16),
            pltpu.VMEM((n,) + keys.shape, jnp.bfloat16),
            pltpu.VMEM((n,) + values.shape, jnp.bfloat16),
            pltpu.VMEM((kv_heads, 2, tall, HEAD_SIZE), jnp.bfloat16),
            pltpu.VMEM((kv_heads, 2, tall, span), jnp.bfloat16),
            pltpu.VMEM((kv_heads, 2, tall, HEAD_SIZE), jnp.float32),
            pltpu.VMEM((kv_heads, 2, tall, 2 * HEAD_SIZE), jnp.float32),
            pltpu.SemaphoreType.DMA((4,)),
            pltpu.SemaphoreType.DMA((2, 2, n)),
            pltpu.SemaphoreType.DMA((2, 2, n)),
        ],
        compiler_params=pltpu.CompilerParams(
            collective_id=0, has_side_effects=True, vmem_limit_bytes=32 * 2**20
        ),
    )(*inputs)


def solution(mesh):
    split = P(("groups", "ctx"), ("head", "rep"))
    return jax.shard_map(
        functools.partial(shards, mesh.shape["ctx"]),
        mesh=mesh,
        in_specs=(split, split, split, P()),
        out_specs=split,
        check_vma=False,
    )
```

time: 27.7 us -> 23.8 us (0.86)
  Pallas kernels: 25.7 us -> 22.9 us
  local copies, waits for them, and re-layouts: 1.87 us -> 0.8 us
    pallas_call x1, Pallas kernels: 25.7 us -> 22.9 us  [shards(): pl.pallas_call(functools.partial(attend, n), out_shape=jax.ShapeDtypeStru...]
    unnamed x1, local copies, waits for them, and re-layouts: 1.87 us -> 0.8 us
where the time goes in v2:
time: 23.8 us; the launch traced here: 23.7 us
  Pallas kernels  22.9 us (96%)
  local copies, waits for them, and re-layouts  0.8 us (3%)
    pallas_call x1, Pallas kernels, shards(): pl.pallas_call(functools.partial(attend, n), out_shape=jax.ShapeDtypeStru...  22.9 us
    unnamed x1, local copies, waits for them, and re-layouts  0.8 us

profile of v2, /device:TPU:0, one launch (start us, length us, event | category | flops | bytes accessed | tf_op | source)
XLA Modules:
  0.0 23.7 jit_solution(14800667227633123744)
XLA Ops:
  0.0 22.9 %shard_map.46 = bf16[256,1024]{1,0:T(8,128)(2,1)S(1)} custom-call(s32[8]{0:T(128)} %order_hbm.1, bf16[256,1024]{1,0:T(8,128)(2,1)} %q_hbm.1, bf16[256,256]{1,0:T(8,128)(2,1)} %k_hbm.1, bf16[256,256]{1,0:T(8,128)(2,1)} %v_hbm.1), custom_call_target="tpu_custom_call" | custom-call | tf_op jit(solution)/shard_map/pallas_call | solution.py:224
  22.9 0.8 %copy.6 = bf16[256,1024]{1,0:T(8,128)(2,1)} copy(bf16[256,1024]{1,0:T(8,128)(2,1)S(1)} %shard_map.46) | data formatting | bytes 1048576

commit v3 on v2

--- a/solution.py
+++ b/solution.py
@@ -22,17 +22,27 @@
     me = lax.axis_index("ctx")
     rows, q_cols = q_ref.shape
     span = rows // 2
-    kv_heads = k_ref.shape[2] // HEAD_SIZE
+    kv_heads = k_ref.shape[1]
     group = q_cols // HEAD_SIZE // kv_heads
     exponent_scale = math.log2(math.e) / math.sqrt(HEAD_SIZE)
     buffers = (k_ref, v_ref)
 
-    load_k = pltpu.make_async_copy(k_hbm, k_ref.at[me], load_sem.at[0])
-    load_v = pltpu.make_async_copy(v_hbm, v_ref.at[me], load_sem.at[1])
-    load_order = pltpu.make_async_copy(order_hbm, order_ref, load_sem.at[3])
-    load_q = pltpu.make_async_copy(q_hbm, q_ref, load_sem.at[2])
-    load_k.start()
-    load_v.start()
+    def columns(head):
+        return pl.ds(head * HEAD_SIZE, HEAD_SIZE)
+
+    pieces = [(kind, head) for kind in (KEY, VALUE) for head in range(kv_heads)]
+    loads = [
+        pltpu.make_async_copy(
+            (k_hbm, v_hbm)[kind].at[:, columns(head)],
+            buffers[kind].at[me, head],
+            load_sem.at[kind * kv_heads + head],
+        )
+        for kind, head in pieces
+    ]
+    load_order = pltpu.make_async_copy(order_hbm, order_ref, load_sem.at[2 * kv_heads])
+    load_q = pltpu.make_async_copy(q_hbm, q_ref, load_sem.at[2 * kv_heads + 1])
+    for load in loads:
+        load.start()
     load_q.start()
     load_order.start()
 
@@ -49,40 +59,38 @@
 
     pl.semaphore_wait(barrier, jnp.where(me > 0, 1, 0) + jnp.where(me < n - 1, 1, 0))
 
-    def hop(way, kind, step, block):
+    def hop(way, kind, head, step, block):
         lane = (way + 1) // 2
+        piece = kind * kv_heads + head
         return pltpu.make_async_remote_copy(
-            src_ref=buffers[kind].at[block],
-            dst_ref=buffers[kind].at[block],
-            send_sem=send_sem.at[lane, kind, step],
-            recv_sem=recv_sem.at[lane, kind, step],
+            src_ref=buffers[kind].at[block, head],
+            dst_ref=buffers[kind].at[block, head],
+            send_sem=send_sem.at[lane, piece, step],
+            recv_sem=recv_sem.at[lane, piece, step],
             device_id={"ctx": jnp.clip(me + way, 0, n - 1)},
             device_id_type=MESH,
         )
 
-    def arrive(kind, step):
+    def arrive(kind, head, step):
         for way in (major, -major):
             @pl.when(inside(me - way * step))
             def _():
-                hop(way, kind, step - 1, me - way * step).wait_recv()
+                hop(way, kind, head, step - 1, me - way * step).wait_recv()
 
                 @pl.when(inside(me + way))
                 def _():
-                    hop(way, kind, step, me - way * step).start()
-
-    for kind, load in ((KEY, load_k), (VALUE, load_v)):
+                    hop(way, kind, head, step, me - way * step).start()
+
+    for (kind, head), load in zip(pieces, loads):
         load.wait()
         for way in (major, -major):
             @pl.when(inside(me + way))
             def _():
-                hop(way, kind, 0, me).start()
+                hop(way, kind, head, 0, me).start()
 
     load_q.wait()
     load_order.wait()
 
-    def columns(head):
-        return pl.ds(head * HEAD_SIZE, HEAD_SIZE)
-
     def low_first(block):
         return order_ref[2 * block] < order_ref[2 * block + 1]
 
@@ -90,7 +98,7 @@
         return jnp.minimum(order_ref[2 * block], order_ref[2 * block + 1])
 
     def low_high(ref, block, head):
-        first, second = ref[block, :span, columns(head)], ref[block, span:, columns(head)]
+        first, second = ref[block, head, :span], ref[block, head, span:]
         swap = low_first(block)
         return jnp.where(swap, first, second), jnp.where(swap, second, first)
 
@@ -141,61 +149,37 @@
             weights_of(high, high_top), value_high
         )
 
-    def weigh(block):
+    def weigh(block, head):
         earlier = low_span(block) < low_span(me)
-        for head in range(kv_heads):
-            key_low, key_high = low_high(k_ref, block, head)
-            cross = score(head, 1, key_low)
-            other = score(
-                head,
-                jnp.where(earlier, stack_ref[head, 0], stack_ref[head, 1]),
-                jnp.where(earlier, key_low, key_high),
-            )
-            other_top = peak(other)
-            old_low, old_high = top_ref[head, 0][:, :1], top_ref[head, 1][:, :1]
-            low_top = jnp.maximum(old_low, jnp.where(earlier, other_top, MASKED))
-            high_top = jnp.maximum(
-                jnp.maximum(old_high, peak(cross)), jnp.where(earlier, MASKED, other_top)
-            )
-            keep(top_ref.at[head, 0], low_top)
-            keep(top_ref.at[head, 1], high_top)
-            acc_ref[head, 0] *= jnp.exp2((old_low - low_top) * exponent_scale)
-            acc_ref[head, 1] *= jnp.exp2((old_high - high_top) * exponent_scale)
-            p_ref[head, 0] = weights_of(cross, high_top)
-            p_ref[head, 1] = weights_of(other, jnp.where(earlier, low_top, high_top))
-
-    def gather(block):
+        key_low, key_high = low_high(k_ref, block, head)
+        cross = score(head, 1, key_low)
+        other = score(
+            head,
+            jnp.where(earlier, stack_ref[head, 0], stack_ref[head, 1]),
+            jnp.where(earlier, key_low, key_high),
+        )
+        other_top = peak(other)
+        old_low, old_high = top_ref[head, 0][:, :1], top_ref[head, 1][:, :1]
+        low_top = jnp.maximum(old_low, jnp.where(earlier, other_top, MASKED))
+        high_top = jnp.maximum(
+            jnp.maximum(old_high, peak(cross)), jnp.where(earlier, MASKED, other_top)
+        )
+        keep(top_ref.at[head, 0], low_top)
+        keep(top_ref.at[head, 1], high_top)
+        acc_ref[head, 0] *= jnp.exp2((old_low - low_top) * exponent_scale)
+        acc_ref[head, 1] *= jnp.exp2((old_high - high_top) * exponent_scale)
+        p_ref[head, 0] = weights_of(cross, high_top)
+        p_ref[head, 1] = weights_of(other, jnp.where(earlier, low_top, high_top))
+
+    def gather(block, head):
         earlier = low_span(block) < low_span(me)
-        for head in range(kv_heads):
-            value_low, value_high = low_high(v_ref, block, head)
-            cross = product(p_ref[head, 0], value_low)
-            other = product(p_ref[head, 1], jnp.where(earlier, value_low, value_high))
-            acc_ref[head, 0] += jnp.where(earlier, other, 0.0)
-            acc_ref[head, 1] += cross + jnp.where(earlier, 0.0, other)
-
-    def turn(step, carry):
-        arrive(KEY, step)
-
-        @pl.when(inside(me - major * step))
-        def _():
-            weigh(me - major * step)
-
-        arrive(VALUE, step)
-
-        @pl.when(inside(me - major * step))
-        def _():
-            gather(me - major * step)
-
-        @pl.when(inside(me + major * step))
-        def _():
-            weigh(me + major * step)
-            gather(me + major * step)
-
-        return carry
-
-    lax.fori_loop(1, n, turn, 0)
-
-    for head in range(kv_heads):
+        value_low, value_high = low_high(v_ref, block, head)
+        cross = product(p_ref[head, 0], value_low)
+        other = product(p_ref[head, 1], jnp.where(earlier, value_low, value_high))
+        acc_ref[head, 0] += jnp.where(earlier, other, 0.0)
+        acc_ref[head, 1] += cross + jnp.where(earlier, 0.0, other)
+
+    def finish(head):
         for member in range(group):
             column = columns(head * group + member)
             part = pl.ds(member * span, span)
@@ -204,12 +188,34 @@
             out_ref[:span, column] = jnp.where(mine_first, low, high).astype(out_ref.dtype)
             out_ref[span:, column] = jnp.where(mine_first, high, low).astype(out_ref.dtype)
 
+    def turn(step, last=False):
+        for kind, work in ((KEY, weigh), (VALUE, gather)):
+            for head in range(kv_heads):
+                arrive(kind, head, step)
+
+                @pl.when(inside(me - major * step))
+                def _():
+                    work(me - major * step, head)
+
+                if last and kind == VALUE:
+                    finish(head)
+
+        if not last:
+            @pl.when(inside(me + major * step))
+            def _():
+                for head in range(kv_heads):
+                    weigh(me + major * step, head)
+                    gather(me + major * step, head)
+
+    lax.fori_loop(1, n - 1, lambda step, carry: turn(step) or carry, 0)
+    turn(n - 1, last=True)
+
     def drain(step, carry):
-        for kind in (KEY, VALUE):
+        for kind, head in pieces:
             for way in (major, -major):
                 @pl.when(inside(me - way * step) & inside(me + way))
                 def _():
-                    hop(way, kind, step, me - way * step).wait_send()
+                    hop(way, kind, head, step, me - way * step).wait_send()
         return carry
 
     lax.fori_loop(0, n - 1, drain, 0)
@@ -229,15 +235,15 @@
         scratch_shapes=[
             pltpu.SMEM(span_order.shape, jnp.int32),
             pltpu.VMEM((rows, q_cols), jnp.bfloat16),
-            pltpu.VMEM((n,) + keys.shape, jnp.bfloat16),
-            pltpu.VMEM((n,) + values.shape, jnp.bfloat16),
+            pltpu.VMEM((n, kv_heads, rows, HEAD_SIZE), jnp.bfloat16),
+            pltpu.VMEM((n, kv_heads, rows, HEAD_SIZE), jnp.bfloat16),
             pltpu.VMEM((kv_heads, 2, tall, HEAD_SIZE), jnp.bfloat16),
             pltpu.VMEM((kv_heads, 2, tall, span), jnp.bfloat16),
             pltpu.VMEM((kv_heads, 2, tall, HEAD_SIZE), jnp.float32),
             pltpu.VMEM((kv_heads, 2, tall, 2 * HEAD_SIZE), jnp.float32),
-            pltpu.SemaphoreType.DMA((4,)),
-            pltpu.SemaphoreType.DMA((2, 2, n)),
-            pltpu.SemaphoreType.DMA((2, 2, n)),
+            pltpu.SemaphoreType.DMA((2 * kv_heads + 2,)),
+            pltpu.SemaphoreType.DMA((2, 2 * kv_heads, n)),
+            pltpu.SemaphoreType.DMA((2, 2 * kv_heads, n)),
         ],
         compiler_params=pltpu.CompilerParams(
             collective_id=0, has_side_effects=True, vmem_limit_bytes=32 * 2**20

time: 23.8 us -> 23.9 us (level)
  no operation moved by 1% of the time
where the time goes in v3:
time: 23.9 us; the launch traced here: 23.8 us
  Pallas kernels  23 us (96%)
  local copies, waits for them, and re-layouts  0.8 us (3%)
    pallas_call x1, Pallas kernels, shards(): pl.pallas_call(functools.partial(attend, n), out_shape=jax.ShapeDtypeStru...  23 us
    unnamed x1, local copies, waits for them, and re-layouts  0.8 us

profile of v3, /device:TPU:0, one launch (start us, length us, event | category | flops | bytes accessed | tf_op | source)
XLA Modules:
  0.0 23.8 jit_solution(10244600236196389564)
XLA Ops:
  0.0 23.0 %shard_map.46 = bf16[256,1024]{1,0:T(8,128)(2,1)S(1)} custom-call(s32[8]{0:T(128)} %order_hbm.1, bf16[256,1024]{1,0:T(8,128)(2,1)} %q_hbm.1, bf16[256,256]{1,0:T(8,128)(2,1)} %k_hbm.1, bf16[256,256]{1,0:T(8,128)(2,1)} %v_hbm.1), custom_call_target="tpu_custom_call" | custom-call | tf_op jit(solution)/shard_map/pallas_call | solution.py:230
  23.0 0.8 %copy.6 = bf16[256,1024]{1,0:T(8,128)(2,1)} copy(bf16[256,1024]{1,0:T(8,128)(2,1)S(1)} %shard_map.46) | data formatting | bytes 1048576

commit v4 on v2

--- a/solution.py
+++ b/solution.py
@@ -16,7 +16,7 @@
 
 def attend(
     n, order_hbm, q_hbm, k_hbm, v_hbm, out_ref,
-    order_ref, q_ref, k_ref, v_ref, stack_ref, p_ref, top_ref, acc_ref,
+    order_ref, q_ref, k_ref, v_ref, stack_ref, p_ref, top_ref, total_ref, acc_ref,
     load_sem, send_sem, recv_sem,
 ):
     me = lax.axis_index("ctx")
@@ -109,11 +109,10 @@
     def keep(ref, value):
         ref[...] = jnp.broadcast_to(value, (group * span, HEAD_SIZE))
 
-    def with_ones(values):
-        return jnp.concatenate([values, jnp.ones_like(values)], axis=1)
-
     def product(weights, values):
-        return jnp.dot(weights, with_ones(values), preferred_element_type=jnp.float32)
+        return jnp.dot(weights, values, preferred_element_type=jnp.float32)
+
+    ones = jnp.ones((span, HEAD_SIZE), jnp.bfloat16)
 
     mine_first = low_first(me)
     for head in range(kv_heads):
@@ -132,14 +131,16 @@
         low = score(head, 0, key_low) + bias
         low_top = peak(low)
         keep(top_ref.at[head, 0], low_top)
-        acc_ref[head, 0] = product(weights_of(low, low_top), value_low)
+        low_weights = weights_of(low, low_top)
+        total_ref[head, 0] = product(low_weights, ones)
+        acc_ref[head, 0] = product(low_weights, value_low)
         cross = score(head, 1, key_low)
         high = score(head, 1, key_high) + bias
         high_top = jnp.maximum(peak(cross), peak(high))
         keep(top_ref.at[head, 1], high_top)
-        acc_ref[head, 1] = product(weights_of(cross, high_top), value_low) + product(
-            weights_of(high, high_top), value_high
-        )
+        cross_weights, high_weights = weights_of(cross, high_top), weights_of(high, high_top)
+        total_ref[head, 1] = product(cross_weights, ones) + product(high_weights, ones)
+        acc_ref[head, 1] = product(cross_weights, value_low) + product(high_weights, value_high)
 
     def weigh(block):
         earlier = low_span(block) < low_span(me)
@@ -159,10 +160,19 @@
             )
             keep(top_ref.at[head, 0], low_top)
             keep(top_ref.at[head, 1], high_top)
-            acc_ref[head, 0] *= jnp.exp2((old_low - low_top) * exponent_scale)
-            acc_ref[head, 1] *= jnp.exp2((old_high - high_top) * exponent_scale)
-            p_ref[head, 0] = weights_of(cross, high_top)
-            p_ref[head, 1] = weights_of(other, jnp.where(earlier, low_top, high_top))
+            low_alpha = jnp.exp2((old_low - low_top) * exponent_scale)
+            high_alpha = jnp.exp2((old_high - high_top) * exponent_scale)
+            cross_weights = weights_of(cross, high_top)
+            other_weights = weights_of(other, jnp.where(earlier, low_top, high_top))
+            cross_total, other_total = product(cross_weights, ones), product(other_weights, ones)
+            p_ref[head, 0] = cross_weights
+            p_ref[head, 1] = other_weights
+            acc_ref[head, 0] *= low_alpha
+            acc_ref[head, 1] *= high_alpha
+            total_ref[head, 0] = total_ref[head, 0] * low_alpha + jnp.where(earlier, other_total, 0.0)
+            total_ref[head, 1] = (
+                total_ref[head, 1] * high_alpha + cross_total + jnp.where(earlier, 0.0, other_total)
+            )
 
     def gather(block):
         earlier = low_span(block) < low_span(me)
@@ -173,34 +183,36 @@
             acc_ref[head, 0] += jnp.where(earlier, other, 0.0)
             acc_ref[head, 1] += cross + jnp.where(earlier, 0.0, other)
 
-    def turn(step, carry):
+    def turn(step, last=False):
         arrive(KEY, step)
 
         @pl.when(inside(me - major * step))
         def _():
             weigh(me - major * step)
 
+        if last:
+            total_ref[...] = 1.0 / total_ref[...]
         arrive(VALUE, step)
 
         @pl.when(inside(me - major * step))
         def _():
             gather(me - major * step)
 
-        @pl.when(inside(me + major * step))
-        def _():
-            weigh(me + major * step)
-            gather(me + major * step)
-
-        return carry
-
-    lax.fori_loop(1, n, turn, 0)
+        if not last:
+            @pl.when(inside(me + major * step))
+            def _():
+                weigh(me + major * step)
+                gather(me + major * step)
+
+    lax.fori_loop(1, n - 1, lambda step, carry: turn(step) or carry, 0)
+    turn(n - 1, last=True)
 
     for head in range(kv_heads):
         for member in range(group):
             column = columns(head * group + member)
             part = pl.ds(member * span, span)
-            low = acc_ref[head, 0, part, :HEAD_SIZE] / acc_ref[head, 0, part, HEAD_SIZE:]
-            high = acc_ref[head, 1, part, :HEAD_SIZE] / acc_ref[head, 1, part, HEAD_SIZE:]
+            low = acc_ref[head, 0, part] * total_ref[head, 0, part]
+            high = acc_ref[head, 1, part] * total_ref[head, 1, part]
             out_ref[:span, column] = jnp.where(mine_first, low, high).astype(out_ref.dtype)
             out_ref[span:, column] = jnp.where(mine_first, high, low).astype(out_ref.dtype)
 
@@ -234,7 +246,8 @@
             pltpu.VMEM((kv_heads, 2, tall, HEAD_SIZE), jnp.bfloat16),
             pltpu.VMEM((kv_heads, 2, tall, span), jnp.bfloat16),
             pltpu.VMEM((kv_heads, 2, tall, HEAD_SIZE), jnp.float32),
-            pltpu.VMEM((kv_heads, 2, tall, 2 * HEAD_SIZE), jnp.float32),
+            pltpu.VMEM((kv_heads, 2, tall, HEAD_SIZE), jnp.float32),
+            pltpu.VMEM((kv_heads, 2, tall, HEAD_SIZE), jnp.float32),
             pltpu.SemaphoreType.DMA((4,)),
             pltpu.SemaphoreType.DMA((2, 2, n)),
             pltpu.SemaphoreType.DMA((2, 2, n)),

time: 23.8 us -> 23.8 us (level)
  no operation moved by 1% of the time
where the time goes in v4:
time: 23.8 us; the launch traced here: 23.7 us
  Pallas kernels  22.9 us (96%)
  local copies, waits for them, and re-layouts  0.8 us (3%)
    pallas_call x1, Pallas kernels, shards(): pl.pallas_call(functools.partial(attend, n), out_shape=jax.ShapeDtypeStru...  22.9 us
    unnamed x1, local copies, waits for them, and re-layouts  0.8 us

profile of v4, /device:TPU:0, one launch (start us, length us, event | category | flops | bytes accessed | tf_op | source)
XLA Modules:
  0.0 23.7 jit_solution(1998129225825199709)
XLA Ops:
  0.0 22.9 %shard_map.46 = bf16[256,1024]{1,0:T(8,128)(2,1)S(1)} custom-call(s32[8]{0:T(128)} %order_hbm.1, bf16[256,1024]{1,0:T(8,128)(2,1)} %q_hbm.1, bf16[256,256]{1,0:T(8,128)(2,1)} %k_hbm.1, bf16[256,256]{1,0:T(8,128)(2,1)} %v_hbm.1), custom_call_target="tpu_custom_call" | custom-call | tf_op jit(solution)/shard_map/pallas_call | solution.py:236
  22.9 0.8 %copy.6 = bf16[256,1024]{1,0:T(8,128)(2,1)} copy(bf16[256,1024]{1,0:T(8,128)(2,1)S(1)} %shard_map.46) | data formatting | bytes 1048576
